TPU v7x, 32 devices: a whole 2x2x4 slice. The times are simulated.
32 devices in a mesh: row: 8 (over z, x), col: 4 (over y, core).
Axes of the slice: x: 2, y: 2, z: 4, core: 2. Of those that a mesh axis runs over, the one named last changes fastest.
Arguments:
- curvature: float32 [32, 1024, 4096], P(None, 'row', 'col'), may hold values from -4 to 7, as said below
Outputs:
- factored: float32 [32, 1024, 4096], P(None, 'row', 'col')
Inputs may be any that keep to these rules, and one draw needn't show every extreme that they name: `curvature`: rows 0 to 4095, read as a square matrix, are symmetric positive definite with smallest eigenvalue at least 0.5.
All inputs are finite; a program needn't handle non-finite values.
Results may differ from a plain program's by a relative error of at most 0.0014.
Values may be sent and summed in bfloat16 or wider, within the bound.
A program may use at most 192 MiB of HBM per device.

v0:
```python
import jax
import jax.numpy as jnp
from jax import lax
from jax.sharding import PartitionSpec as P

BLOCK = 128
HIGH = lax.Precision.HIGH
HIGHEST = lax.Precision.HIGHEST


def from_root(x, axis, root):
    mine = lax.axis_index(axis) == root
    return lax.psum(jnp.where(mine, x, jnp.zeros_like(x)), axis)


def nt(left, right, precision=None):
    return lax.dot_general(
        left,
        right,
        (((1,), (1,)), ((), ())),
        precision=precision,
        preferred_element_type=jnp.float32,
    )


def nn(left, right):
    return lax.dot_general(
        left, right, (((1,), (0,)), ((), ())), precision=HIGHEST, preferred_element_type=jnp.float32
    )


def factor_and_inverse(block):
    n = block.shape[0]
    width = min(BLOCK, n)
    rest = 0.5 * (block + block.T)
    identity = jnp.eye(width, dtype=jnp.float32)
    columns, inverses = ([], [])
    for start in range(0, n, width):
        small = lax.linalg.cholesky(rest[:width, :width], symmetrize_input=False)
        inverse = jax.scipy.linalg.solve_triangular(small, identity, lower=True)
        inverses.append(inverse)
        pieces = [jnp.zeros((start, width), jnp.float32)] if start else []
        pieces.append(small)
        if start + width < n:
            below = nt(rest[width:, :width], inverse, HIGHEST)
            rest = rest[width:, width:] - nt(below, below, HIGHEST)
            pieces.append(below)
        columns.append(jnp.concatenate(pieces, 0))
    factor = jnp.concatenate(columns, 1)
    size = width
    while len(inverses) > 1:
        merged = []
        for i in range(0, len(inverses), 2):
            top, bottom = (inverses[i], inverses[i + 1])
            at = i * size
            corner = factor[at + size : at + 2 * size, at : at + size]
            left = -nn(bottom, nn(corner, top))
            merged.append(
                jnp.concatenate(
                    [
                        jnp.concatenate([top, jnp.zeros_like(top)], 1),
                        jnp.concatenate([left, bottom], 1),
                    ],
                    0,
                )
            )
        inverses = merged
        size *= 2
    return (factor, inverses[0])


def on_device(curvature):
    cycles, tile, width = curvature.shape
    row = lax.axis_index("row")
    col = lax.axis_index("col")

    def gather_rows(piece):
        return lax.all_gather(piece, "row", axis=0, tiled=True)

    def own_rows(matrix):
        return lax.dynamic_slice_in_dim(matrix, row * tile, tile, 0)

    block00 = gather_rows(from_root(curvature[0], "col", 0))
    head = from_root(jnp.stack([curvature[0], curvature[1]], 0), "col", 1)
    block01 = gather_rows(head[0])
    block11 = gather_rows(head[1])
    mine0 = gather_rows(curvature[0])
    mine1 = gather_rows(curvature[1])
    factor0, inverse0 = factor_and_inverse(block00)
    below = curvature[1:].reshape((cycles - 1) * tile, width)
    solved0 = nt(below, inverse0, HIGH)
    sent0 = solved0.astype(jnp.bfloat16)
    sent0, block11, block01 = lax.optimization_barrier((sent0, block11, block01))
    panel0 = from_root(sent0, "col", 0)
    next0 = nn(inverse0, block01).astype(jnp.bfloat16)
    facing0 = nn(inverse0, mine0).astype(jnp.bfloat16)

    def tn(left, right):
        return lax.dot_general(
            left, right, (((0,), (0,)), ((), ())), preferred_element_type=jnp.float32
        )

    factor1, inverse1 = factor_and_inverse(block11 - tn(next0, next0))
    facing1 = nn(inverse1, mine1 - tn(next0, facing0)).astype(jnp.bfloat16)

    def plain(left, right):
        return lax.dot_general(
            left, right, (((1,), (0,)), ((), ())), preferred_element_type=jnp.float32
        )

    state = jnp.where(col == 0, solved0, below - plain(panel0, facing0))
    low = state[tile:]
    solved1 = nt(low, inverse1, HIGH)
    panel1 = from_root(solved1.astype(jnp.bfloat16), "col", 1)
    low = jnp.where(col == 1, solved1, jnp.where(col > 1, low - plain(panel1, facing1), low))
    zeros = jnp.zeros((tile, width), jnp.float32)
    first = jnp.where(col == 0, own_rows(factor0), zeros)
    second = jnp.where(col == 0, state[:tile], jnp.where(col == 1, own_rows(factor1), zeros))
    return jnp.concatenate([first, second, low], 0).reshape(cycles, tile, width)


def solution(mesh):
    in_specs = (P(None, "row", "col"),)
    out_specs = P(None, "row", "col")
    return jax.shard_map(
        on_device, mesh=mesh, in_specs=in_specs, out_specs=out_specs, check_vma=False
    )
```

profile of v0, /device:TPU:1, one launch (start us, length us, event | category | flops | bytes accessed | tf_op | source)
XLA Modules:
  0.0 980.9 jit_solution(16894256061563243643)
XLA Ops:
  11.2 45.0 %all-reduce.25.cloned.1.call-done = (f32[128,1024]{0,1:T(8,128)}, f32[2,128,1024]{1,2,0:T(8,128)}) async-done(((f32[128,1024]{0,1:T(8,128)}, f32[2,128,1024]{1,2,0:T(8,128)}), (f32[128,1024]{0,1:T(8,128)}, f32[2,128,1024]{1,2,0:T(8,128)})) %all-reduce.25.cloned.1.call-update) | async-done | bytes 1572880 | tf_op jit(solution)/shard_map/psum | solution.py:13
  59.8 11.9 %slice.227 = f32[31,128,1024]{2,1,0:T(8,128)} slice(f32[32,128,1024]{2,1,0:T(8,128)} %param.4), slice={[1:32], [0:128], [0:1024]} | slice | bytes 32505856 | tf_op jit(solution)/shard_map/slice | solution.py:90
  71.7 60.6 %all-gather.10.cloned.1.call-done = f32[1024,1024]{0,1:T(8,128)} async-done(((f32[128,1024]{0,1:T(8,128)}), f32[1024,1024]{0,1:T(8,128)}) %all-gather.10.cloned.1.call-update) | async-done | bytes 4194320 | tf_op jit(solution)/shard_map/all_gather | solution.py:78
  144.2 11.7 %custom-call.36 = f32[128,128]{1,0:T(8,128)S(1)} custom-call(f32[128,128]{1,0:T(8,128)S(1)} %slice.260), custom_call_target="Cholesky" | custom-call | tf_op jit(solution)/shard_map/cholesky/custom-call.1 | solution.py:39
  175.5 12.0 %custom-call.38 = f32[128,128]{1,0:T(8,128)S(1)} custom-call(f32[128,128]{1,0:T(8,128)S(1)} %slice.263), custom_call_target="Cholesky" | custom-call | tf_op jit(solution)/shard_map/cholesky/custom-call.1 | solution.py:39
  205.7 11.7 %custom-call.40 = f32[128,128]{1,0:T(8,128)S(1)} custom-call(f32[128,128]{1,0:T(8,128)S(1)} %slice.266), custom_call_target="Cholesky" | custom-call | tf_op jit(solution)/shard_map/cholesky/custom-call.1 | solution.py:39
  235.1 11.7 %custom-call.42 = f32[128,128]{1,0:T(8,128)S(1)} custom-call(f32[128,128]{1,0:T(8,128)S(1)} %slice.269), custom_call_target="Cholesky" | custom-call | tf_op jit(solution)/shard_map/cholesky/custom-call.1 | solution.py:39
  262.6 11.9 %custom-call.44 = f32[128,128]{1,0:T(8,128)S(1)} custom-call(f32[128,128]{1,0:T(8,128)S(1)} %slice.272), custom_call_target="Cholesky" | custom-call | tf_op jit(solution)/shard_map/cholesky/custom-call.1 | solution.py:39
  289.7 11.7 %custom-call.46 = f32[128,128]{1,0:T(8,128)S(1)} custom-call(f32[128,128]{1,0:T(8,128)S(1)} %slice.275), custom_call_target="Cholesky" | custom-call | tf_op jit(solution)/shard_map/cholesky/custom-call.1 | solution.py:39
  315.7 11.7 %custom-call.48 = f32[128,128]{1,0:T(8,128)S(1)} custom-call(f32[128,128]{1,0:T(8,128)S(1)} %slice.278), custom_call_target="Cholesky" | custom-call | tf_op jit(solution)/shard_map/cholesky/custom-call.1 | solution.py:39
  340.1 11.7 %custom-call.50 = f32[128,128]{1,0:T(8,128)S(1)} custom-call(f32[128,128]{1,0:T(8,128)S(1)} %convolution_subtract_fusion.8), custom_call_target="Cholesky" | custom-call | tf_op jit(solution)/shard_map/cholesky/custom-call.1 | solution.py:39
  376.0 31.0 %bitcast_convert_fusion = (bf16[3968,1024]{1,0:T(8,128)(2,1)}, f32[1024,3968]{0,1:T(8,128)}) fusion(f32[3968,1024]{1,0:T(8,128)} %bitcast.189, f32[512,512]{1,0:T(8,128)S(1)} %select_maximum_fusion.3, f32[128,128]{1,0:T(8,128)S(1)} %copy-done.83, f32[128,128]{1,0:T(8,128)S(1)} %convolution_negate_fusion.10, f32[128,256]{1,0:T(8,128)S(1)} %copy-done.64, ...), kind=kOutput, calls=%fused_computation.3 | convolution fusion | flops 24976949248 | bytes 43778048 | tf_op jit(solution)/shard_map/dot_general | solution.py:17
  411.7 19.4 %convolution_convert_fusion = bf16[1024,1024]{1,0:T(8,128)(2,1)S(1)} fusion(f32[1024,1024]{0,1:T(8,128)} %bitcast.192, f32[512,512]{1,0:T(8,128)} %copy-done.31, f32[128,128]{1,0:T(8,128)S(1)} %copy-done.84, f32[128,128]{1,0:T(8,128)S(1)} %convolution_negate_fusion.10, f32[128,256]{1,0:T(8,128)S(1)} %copy-done.65, ...), kind=kOutput, calls=%fused_computation.27 | convolution fusion | flops 12894339072 | bytes 9437184 | tf_op jit(solution)/shard_map/dot_general | solution.py:27
  449.4 11.7 %custom-call.52 = f32[128,128]{1,0:T(8,128)S(1)} custom-call(f32[128,128]{1,0:T(8,128)S(1)} %slice.287), custom_call_target="Cholesky" | custom-call | tf_op jit(solution)/shard_map/cholesky/custom-call.1 | solution.py:39
  481.1 11.9 %custom-call.54 = f32[128,128]{1,0:T(8,128)S(1)} custom-call(f32[128,128]{1,0:T(8,128)S(1)} %slice.290), custom_call_target="Cholesky" | custom-call | tf_op jit(solution)/shard_map/cholesky/custom-call.1 | solution.py:39
  512.5 11.7 %custom-call.56 = f32[128,128]{1,0:T(8,128)S(1)} custom-call(f32[128,128]{1,0:T(8,128)S(1)} %slice.293), custom_call_target="Cholesky" | custom-call | tf_op jit(solution)/shard_map/cholesky/custom-call.1 | solution.py:39
  526.2 10.2 %custom-call.57 = f32[1,128,128]{1,2,0:T(8,128)S(1)} custom-call(f32[1,128,128]{2,1,0:T(8,128)S(1)} %get-tuple-element.25), custom_call_target="InvertDiagBlocksLowerTriangular" | custom-call | tf_op jit(solution)/shard_map/jit(_solve_triangular)/triangular_solve | solution.py:40
  542.7 11.7 %custom-call.58 = f32[128,128]{1,0:T(8,128)S(1)} custom-call(f32[128,128]{1,0:T(8,128)S(1)} %slice.296), custom_call_target="Cholesky" | custom-call | tf_op jit(solution)/shard_map/cholesky/custom-call.1 | solution.py:39
  572.6 11.9 %custom-call.60 = f32[128,128]{1,0:T(8,128)S(1)} custom-call(f32[128,128]{1,0:T(8,128)S(1)} %slice.299), custom_call_target="Cholesky" | custom-call | tf_op jit(solution)/shard_map/cholesky/custom-call.1 | solution.py:39
  601.1 13.2 %custom-call.62 = f32[128,128]{1,0:T(8,128)} custom-call(f32[128,128]{1,0:T(8,128)} %slice.302), custom_call_target="Cholesky" | custom-call | tf_op jit(solution)/shard_map/cholesky/custom-call.1 | solution.py:39
  618.0 11.3 %custom-call.63 = f32[1,128,128]{1,2,0:T(8,128)} custom-call(f32[1,128,128]{2,1,0:T(8,128)} %get-tuple-element.19), custom_call_target="InvertDiagBlocksLowerTriangular" | custom-call | tf_op jit(solution)/shard_map/jit(_solve_triangular)/triangular_solve | solution.py:40
  635.1 13.2 %custom-call.64 = f32[128,128]{1,0:T(8,128)} custom-call(f32[128,128]{1,0:T(8,128)} %slice.305), custom_call_target="Cholesky" | custom-call | tf_op jit(solution)/shard_map/cholesky/custom-call.1 | solution.py:39
  651.8 11.3 %custom-call.65 = f32[1,128,128]{1,2,0:T(8,128)} custom-call(f32[1,128,128]{2,1,0:T(8,128)} %get-tuple-element.17), custom_call_target="InvertDiagBlocksLowerTriangular" | custom-call | tf_op jit(solution)/shard_map/jit(_solve_triangular)/triangular_solve | solution.py:40
  674.4 13.2 %custom-call.66 = f32[128,128]{1,0:T(8,128)} custom-call(f32[128,128]{1,0:T(8,128)} %convolution_subtract_fusion.7), custom_call_target="Cholesky" | custom-call | tf_op jit(solution)/shard_map/cholesky/custom-call.1 | solution.py:39
  691.2 11.6 %custom-call.67 = f32[1,128,128]{1,2,0:T(8,128)} custom-call(f32[1,128,128]{2,1,0:T(8,128)} %get-tuple-element.15), custom_call_target="InvertDiagBlocksLowerTriangular" | custom-call | tf_op jit(solution)/shard_map/jit(_solve_triangular)/triangular_solve | solution.py:40
  720.4 20.0 %fusion.9 = bf16[1024,1024]{1,0:T(8,128)(2,1)} fusion(f32[1,1024,1024]{1,2,0:T(8,128)} %all-gather.16.cloned.1.call-done, f32[512,512]{1,0:T(8,128)} %copy-done.31, f32[128,128]{1,0:T(8,128)} %copy.12, f32[128,128]{1,0:T(8,128)} %copy-done.77, f32[128,256]{1,0:T(8,128)} %concatenate.225, f32[256,256]{1,0:T(8,128)} %copy-done.71, f32[256,512]{1,0:T(8,128)} %copy-done.61, ...), kind=kOutput, calls=%fused_computation.26 | convolution fusion | flops 12894339072 | bytes 9437184 | tf_op jit(solution)/shard_map/dot_general | solution.py:27
  740.3 23.0 %bitcast_select_fusion = f32[3968,1024]{1,0:T(8,128)} fusion(f32[1024,3968]{0,1:T(8,128)} %get-tuple-element.64, f32[3968,1024]{1,0:T(8,128)} %bitcast.190, pred[]{:T(512)S(6)} %eq.47, bf16[3968,1024]{1,0:T(8,128)(2,1)} %all-reduce.21.cloned.1.call-done, bf16[1024,1024]{1,0:T(8,128)(2,1)} %fusion.9), kind=kOutput, calls=%fused_computation.2 | convolution fusion | flops 8329625600 | bytes 58982400 | tf_op jit(solution)/shard_map/dot_general | solution.py:107
  763.4 31.3 %convert_select_fusion = (bf16[3840,1024]{1,0:T(8,128)(2,1)}, f32[3840,1024]{1,0:T(8,128)}) fusion(pred[]{:T(512)S(6)} %eq.49, f32[512,512]{1,0:T(8,128)} %select_maximum_fusion.2, f32[128,128]{1,0:T(8,128)} %copy.27, f32[128,128]{1,0:T(8,128)} %copy-done.81, f32[128,256]{1,0:T(8,128)} %concatenate.258, f32[256,256]{1,0:T(8,128)} %copy-done.72, ...), kind=kOutput, calls=%fused_computation.8 | convolution fusion | flops 24175443968 | bytes 42467328 | tf_op jit(solution)/shard_map/dot_general | solution.py:17
  805.9 17.2 %fusion.3 = bf16[1024,1024]{1,0:T(8,128)(2,1)} fusion(f32[1024,1024]{1,0:T(8,128)} %fusion.249, f32[1,1024,1024]{2,1,0:T(8,128)} %all-gather.18.cloned.1.call-done, f32[512,512]{1,0:T(8,128)S(1)} %copy-done.32, f32[128,128]{1,0:T(8,128)S(1)} %copy-done.86, f32[128,128]{1,0:T(8,128)S(1)} %copy-done.82, f32[128,256]{1,0:T(8,128)S(1)} %copy-done.67, ...), kind=kOutput, calls=%fused_computation.13 | convolution fusion | flops 12894339072 | bytes 13631488 | tf_op jit(solution)/shard_map/dot_general | solution.py:27
  824.4 117.3 %all-reduce.23.cloned.1.call-done = bf16[3840,1024]{1,0:T(8,128)(2,1)} async-done(((bf16[3840,1024]{1,0:T(8,128)(2,1)}), bf16[3840,1024]{1,0:T(8,128)(2,1)}) %all-reduce.23.cloned.1.call-update) | async-done | bytes 7864336 | tf_op jit(solution)/shard_map/psum | solution.py:13
  941.7 20.8 %fusion = f32[3840,1024]{1,0:T(8,128)} fusion(f32[3840,1024]{1,0:T(8,128)} %get-tuple-element.66, f32[3968,1024]{1,0:T(8,128)} %bitcast_select_fusion, bf16[3840,1024]{1,0:T(8,128)(2,1)} %all-reduce.23.cloned.1.call-done, pred[]{:T(512)S(6)} %gt.3, pred[]{:T(512)S(6)} %eq.49, bf16[1024,1024]{1,0:T(8,128)(2,1)} %fusion.3), kind=kOutput, calls=%fused_computation.4 | convolution fusion | flops 8064860160 | bytes 57147392 | tf_op jit(solution)/shard_map/dot_general | solution.py:107
  962.5 11.2 %pad_maximum_fusion = f32[4096,1024]{1,0:T(8,128)} fusion(f32[3840,1024]{1,0:T(8,128)} %fusion, f32[128,1024]{1,0:T(8,128)S(1)} %slice_select_fusion, f32[128,1024]{1,0:T(8,128)S(1)} %dynamic-slice_select_fusion), kind=kLoop, calls=%fused_computation.1 | loop fusion | flops 8388608 | bytes 33554432 | tf_op jit(solution)/shard_map/concatenate | solution.py:119
  (414 shorter events, 319.2 us)
Async XLA Ops:
  6.5 49.7 %all-reduce.25.cloned.1.call-start = ((), (), s32[]{:S(2)}) async-start(), calls=%async_computation.7 | async-start | bytes 3145728 | tf_op jit(solution)/shard_map/psum | solution.py:13
  8.9 49.6 %copy-start.8 = (f32[1,128,1024]{1,2,0:T(8,128)}, f32[1,128,1024]{1,2,0:T(8,128)S(1)}, u32[]{:S(2)}) copy-start(f32[1,128,1024]{1,2,0:T(8,128)S(1)} %copy.46) | copy-start | bytes 1572868
  11.2 121.1 %all-gather.10.cloned.1.call-start = ((), (), s32[]{:S(2)}) async-start(), calls=%async_computation | async-start | bytes 4718592 | tf_op jit(solution)/shard_map/all_gather | solution.py:78
  56.3 350.8 %all-gather.12.cloned.1.call-start = ((), (), s32[]{:S(2)}) async-start(), calls=%async_computation.3 | async-start | bytes 4718592 | tf_op jit(solution)/shard_map/all_gather | solution.py:78
  58.6 348.5 %all-gather.14.cloned.1.call-start = ((), (), s32[]{:S(2)}) async-start(), calls=%async_computation.4 | async-start | bytes 4718592 | tf_op jit(solution)/shard_map/all_gather | solution.py:78
  59.2 661.2 %all-gather.16.cloned.1.call-start = ((), (), s32[]{:S(2)}) async-start(), calls=%async_computation.5 | async-start | bytes 4718592 | tf_op jit(solution)/shard_map/all_gather | solution.py:78
  59.7 680.6 %all-reduce.21.cloned.1.call-start = ((), (), s32[]{:S(2)}) async-start(), calls=%async_computation.1 | async-start | bytes 16252928 | tf_op jit(solution)/shard_map/psum | solution.py:13
  157.2 213.1 %copy-start.44 = (f32[128,128]{1,0:T(8,128)}, f32[128,128]{1,0:T(8,128)S(1)}, u32[]{:S(2)}) copy-start(f32[128,128]{1,0:T(8,128)S(1)} %get-tuple-element.46) | copy-start | bytes 196612
  189.0 178.4 %copy-start.45 = (f32[128,128]{1,0:T(8,128)}, f32[128,128]{1,0:T(8,128)S(1)}, u32[]{:S(2)}) copy-start(f32[128,128]{1,0:T(8,128)S(1)} %get-tuple-element.44) | copy-start | bytes 196612
  262.5 23.0 %copy-start.15 = (f32[512,512]{1,0:T(8,128)}, f32[512,512]{1,0:T(8,128)S(1)}, u32[]{:S(2)}) copy-start(f32[512,512]{1,0:T(8,128)S(1)} %convolution_subtract_fusion.2) | copy-start | bytes 3145732
  275.8 92.1 %copy-start.47 = (f32[128,128]{1,0:T(8,128)}, f32[128,128]{1,0:T(8,128)S(1)}, u32[]{:S(2)}) copy-start(f32[128,128]{1,0:T(8,128)S(1)} %get-tuple-element.38) | copy-start | bytes 196612
  302.7 66.5 %copy-start.40 = (f32[128,128]{1,0:T(8,128)}, f32[128,128]{1,0:T(8,128)S(1)}, u32[]{:S(2)}) copy-start(f32[128,128]{1,0:T(8,128)S(1)} %get-tuple-element.36) | copy-start | bytes 196612
  339.8 32.4 %copy-start.22 = (f32[128,128]{1,0:T(8,128)}, f32[128,128]{1,0:T(8,128)S(1)}, u32[]{:S(2)}) copy-start(f32[128,128]{1,0:T(8,128)S(1)} %fusion.208) | copy-start | bytes 196612
  353.4 13.6 %copy-start.57 = (f32[128,128]{1,0:T(8,128)}, f32[128,128]{1,0:T(8,128)S(1)}, u32[]{:S(2)}) copy-start(f32[128,128]{1,0:T(8,128)S(1)} %copy.10) | copy-start | bytes 196612
  366.8 8.2 copy-start.61
  372.7 38.9 %copy-start.77 = (f32[128,128]{1,0:T(8,128)}, f32[128,128]{1,0:T(8,128)S(1)}, u32[]{:S(2)}) copy-start(f32[128,128]{1,0:T(8,128)S(1)} %convolution_negate_fusion.10) | copy-start | bytes 196612
  373.1 38.5 %copy-start.71 = (f32[256,256]{1,0:T(8,128)}, f32[256,256]{1,0:T(8,128)S(1)}, u32[]{:S(2)}) copy-start(f32[256,256]{1,0:T(8,128)S(1)} %convolution_negate_fusion.4) | copy-start | bytes 786436
  410.8 395.1 %all-gather.18.cloned.1.call-start = ((), (), s32[]{:S(2)}) async-start(), calls=%async_computation.6 | async-start | bytes 4718592 | tf_op jit(solution)/shard_map/all_gather | solution.py:78
  411.6 530.1 %all-reduce.23.cloned.1.call-start = ((), (), s32[]{:S(2)}) async-start(), calls=%async_computation.2 | async-start | bytes 15728640 | tf_op jit(solution)/shard_map/psum | solution.py:13
  411.7 20.8 %copy-start.92 = (f32[1,1024,1024]{1,2,0:T(8,128)S(1)}, f32[1,1024,1024]{1,2,0:T(8,128)}, u32[]{:S(2)}) copy-start(f32[1,1024,1024]{1,2,0:T(8,128)} %all-gather.12.cloned.1.call-done) | copy-start | bytes 12582916
  473.0 7.5 copy-start.25
  505.2 21.0 %copy-start.35 = (f32[128,128]{0,1:T(8,128)}, f32[128,128]{0,1:T(8,128)S(1)}, u32[]{:S(2)}) copy-start(f32[128,128]{0,1:T(8,128)S(1)} %fusion.100) | copy-start | bytes 196612
  566.6 29.7 %copy-start.33 = (f32[128,128]{0,1:T(8,128)}, f32[128,128]{0,1:T(8,128)S(1)}, u32[]{:S(2)}) copy-start(f32[128,128]{0,1:T(8,128)S(1)} %fusion.96) | copy-start | bytes 196612
  706.1 7.6 copy-start.13
  706.1 7.6 copy-start.28
  706.1 7.6 copy-start.38
  706.2 7.6 copy-start.49
  706.2 7.6 copy-start.50
  706.2 7.6 copy-start.69
  706.2 7.6 copy-start.78
  706.2 7.6 copy-start.90
  708.4 8.2 copy-start.62
  (74 other events, 213.1 us)
Sparse Core Ops, SparseCore 0:
  11.3 44.8 all-reduce.24
  58.3 73.9 all-gather.9
  134.3 73.1 all-gather.11
  209.4 74.1 all-gather.13
  285.4 73.3 all-gather.15
  411.0 149.8 all-reduce.20
  563.0 72.3 all-gather.17
  794.8 146.8 all-reduce.22
where the time goes:
time: 993 us; the launch traced here: 981 us
  other arithmetic  423 us (43%)
  matrix products  258 us (26%)
  waiting for transfers between devices  225 us (23%)
  local copies, waits for them, and re-layouts  58.5 us (6%)
  between operations  16.1 us (2%)
    another operation x48, other arithmetic, factor_and_inverse(): small = lax.linalg.cholesky(rest[:width, :width], symmetrize_input=False)  207 us
    another operation x32, other arithmetic, factor_and_inverse(): inverse = jax.scipy.linalg.solve_triangular(small, identity, lower=True)  183 us
    psum x3, waiting for transfers between devices, from_root(): return lax.psum(jnp.where(mine, x, jnp.zeros_like(x)), axis)  162 us
    dot_general x30, matrix products, nt(): lax.dot_general(left, right, (((1,), (1,)), ((), ())), precision=precisio...  117 us
    dot_general x31, matrix products, nn(): lax.dot_general(left, right, (((1,), (0,)), ((), ())), precision=HIGHEST,...  80.8 us
    all_gather x5, waiting for transfers between devices, gather_rows(): return lax.all_gather(piece, 'row', axis=0, tiled=True)  60.6 us
    dot_general x2, matrix products, plain(): lax.dot_general(left, right, (((1,), (0,)), ((), ())), preferred_element_...  43.8 us
    unnamed x196, local copies, waits for them, and re-layouts  21.4 us
  transfers between devices with their start and end apart: 8, of which 3 were waited for; matrix products, arithmetic and copies ran while one was open for 70% of the time, Pallas kernels for 0%

commit v1 on v0

--- a/solution.py
+++ b/solution.py
@@ -10,7 +10,7 @@
 
 def from_root(x, axis, root):
     mine = lax.axis_index(axis) == root
-    return lax.psum(jnp.where(mine, x, jnp.zeros_like(x)), axis)
+    return jnp.sum(lax.all_gather(jnp.where(mine, x, jnp.zeros_like(x)), axis), axis=0)
 
 
 def nt(left, right, precision=None):

time: 993 us -> 1080 us (1.088)
  waiting for transfers between devices: 225 us -> 272 us
  other arithmetic: 423 us -> 469 us
    all_gather x0 -> x4, waiting for transfers between devices: none -> 212 us  [from_root(): lax.all_gather(jnp.where(mine, x, jnp.zeros_like(x)), axis)]
    psum x3 -> x0, waiting for transfers between devices: 162 us -> none  [from_root(): return lax.psum(jnp.where(mine, x, jnp.zeros_like(x)), axis)]
    reduce_sum x0 -> x4, other arithmetic: none -> 36.1 us  [from_root(): jnp.sum(lax.all_gather(jnp.where(mine, x, jnp.zeros_like(x)), axis), axis=0)]
  transfers between devices with their start and end apart: 8 -> 9, of which waited for: 3 -> 4; matrix products, arithmetic and copies ran while one was open for 70% -> 67% of each run, Pallas kernels for 0% -> 0%
where the time goes in v1:
time: 1080 us; the launch traced here: 1070 us
  other arithmetic  469 us (43%)
  waiting for transfers between devices  272 us (25%)
  matrix products  260 us (24%)
  local copies, waits for them, and re-layouts  56.8 us (5%)
  between operations  15.2 us (1%)
    all_gather x4, waiting for transfers between devices, from_root(): lax.all_gather(jnp.where(mine, x, jnp.zeros_like(x)), axis)  212 us
    another operation x48, other arithmetic, factor_and_inverse(): small = lax.linalg.cholesky(rest[:width, :width], symmetrize_input=False)  206 us
    another operation x32, other arithmetic, factor_and_inverse(): inverse = jax.scipy.linalg.solve_triangular(small, identity, lower=True)  184 us
    dot_general x30, matrix products, nt(): lax.dot_general(left, right, (((1,), (1,)), ((), ())), precision=precisio...  117 us
    dot_general x31, matrix products, nn(): lax.dot_general(left, right, (((1,), (0,)), ((), ())), precision=HIGHEST,...  82.4 us
    all_gather x5, waiting for transfers between devices, gather_rows(): return lax.all_gather(piece, 'row', axis=0, tiled=True)  57.8 us
    dot_general x2, matrix products, plain(): lax.dot_general(left, right, (((1,), (0,)), ((), ())), preferred_element_...  43.2 us
    reduce_sum x4, other arithmetic, from_root(): jnp.sum(lax.all_gather(jnp.where(mine, x, jnp.zeros_like(x)), axis), axis=0)  36.1 us
  transfers between devices with their start and end apart: 9, of which 4 were waited for; matrix products, arithmetic and copies ran while one was open for 67% of the time, Pallas kernels for 0%

profile of v1, /device:TPU:1, one launch (start us, length us, event | category | flops | bytes accessed | tf_op | source)
XLA Modules:
  0.0 1073.2 jit_solution(7713912423588243692)
XLA Ops:
  11.5 22.7 %all-gather.17.cloned.1.call-done = f32[4,128,1024]{2,1,0:T(8,128)} async-done(((f32[1,128,1024]{2,1,0:T(8,128)}), f32[4,128,1024]{2,1,0:T(8,128)}) %all-gather.17.cloned.1.call-update) | async-done | bytes 2097168 | tf_op jit(solution)/shard_map/all_gather | solution.py:13
  37.2 33.1 %all-gather.21.cloned.1.call-done = f32[8,128,1024]{2,1,0:T(8,128)} async-done(((f32[2,128,1024]{2,1,0:T(8,128)}), f32[8,128,1024]{2,1,0:T(8,128)}) %all-gather.21.cloned.1.call-update) | async-done | bytes 4194320 | tf_op jit(solution)/shard_map/all_gather | solution.py:13
  76.2 11.9 %slice.227 = f32[31,128,1024]{2,1,0:T(8,128)} slice(f32[32,128,1024]{2,1,0:T(8,128)} %param.4), slice={[1:32], [0:128], [0:1024]} | slice | bytes 32505856 | tf_op jit(solution)/shard_map/slice | solution.py:90
  88.1 57.8 %all-gather.19.cloned.1.call-done = f32[1024,1024]{0,1:T(8,128)} async-done(((f32[128,1024]{0,1:T(8,128)}), f32[1024,1024]{0,1:T(8,128)}) %all-gather.19.cloned.1.call-update) | async-done | bytes 4194320 | tf_op jit(solution)/shard_map/all_gather | solution.py:78
  158.1 11.7 %custom-call.36 = f32[128,128]{1,0:T(8,128)S(1)} custom-call(f32[128,128]{1,0:T(8,128)S(1)} %slice.260), custom_call_target="Cholesky" | custom-call | tf_op jit(solution)/shard_map/cholesky/custom-call.1 | solution.py:39
  189.4 11.9 %custom-call.38 = f32[128,128]{1,0:T(8,128)S(1)} custom-call(f32[128,128]{1,0:T(8,128)S(1)} %slice.263), custom_call_target="Cholesky" | custom-call | tf_op jit(solution)/shard_map/cholesky/custom-call.1 | solution.py:39
  219.3 11.7 %custom-call.40 = f32[128,128]{1,0:T(8,128)S(1)} custom-call(f32[128,128]{1,0:T(8,128)S(1)} %slice.266), custom_call_target="Cholesky" | custom-call | tf_op jit(solution)/shard_map/cholesky/custom-call.1 | solution.py:39
  249.1 11.7 %custom-call.42 = f32[128,128]{1,0:T(8,128)S(1)} custom-call(f32[128,128]{1,0:T(8,128)S(1)} %slice.269), custom_call_target="Cholesky" | custom-call | tf_op jit(solution)/shard_map/cholesky/custom-call.1 | solution.py:39
  276.4 11.9 %custom-call.44 = f32[128,128]{1,0:T(8,128)S(1)} custom-call(f32[128,128]{1,0:T(8,128)S(1)} %slice.272), custom_call_target="Cholesky" | custom-call | tf_op jit(solution)/shard_map/cholesky/custom-call.1 | solution.py:39
  304.3 11.7 %custom-call.46 = f32[128,128]{1,0:T(8,128)S(1)} custom-call(f32[128,128]{1,0:T(8,128)S(1)} %slice.275), custom_call_target="Cholesky" | custom-call | tf_op jit(solution)/shard_map/cholesky/custom-call.1 | solution.py:39
  330.7 11.7 %custom-call.48 = f32[128,128]{1,0:T(8,128)S(1)} custom-call(f32[128,128]{1,0:T(8,128)S(1)} %slice.278), custom_call_target="Cholesky" | custom-call | tf_op jit(solution)/shard_map/cholesky/custom-call.1 | solution.py:39
  357.4 11.7 %custom-call.50 = f32[128,128]{1,0:T(8,128)S(1)} custom-call(f32[128,128]{1,0:T(8,128)S(1)} %convolution_subtract_fusion.8), custom_call_target="Cholesky" | custom-call | tf_op jit(solution)/shard_map/cholesky/custom-call.1 | solution.py:39
  391.4 31.0 %bitcast_convert_fusion = (bf16[3968,1024]{1,0:T(8,128)(2,1)}, f32[1024,3968]{0,1:T(8,128)}) fusion(f32[3968,1024]{1,0:T(8,128)} %bitcast.192, f32[512,512]{1,0:T(8,128)S(1)} %select_maximum_fusion.3, f32[128,128]{1,0:T(8,128)S(1)} %copy-done.77, f32[128,128]{1,0:T(8,128)S(1)} %convolution_negate_fusion.10, f32[128,256]{1,0:T(8,128)S(1)} %copy-done.61, ...), kind=kOutput, calls=%fused_computation.3 | convolution fusion | flops 24976949248 | bytes 43778048 | tf_op jit(solution)/shard_map/dot_general | solution.py:17
  427.0 20.2 %fusion.9 = bf16[1024,1024]{1,0:T(8,128)(2,1)} fusion(f32[1,1024,1024]{2,1,0:T(8,128)} %all-gather.29.cloned.1.call-done, f32[512,512]{1,0:T(8,128)} %copy-done.28, f32[128,128]{1,0:T(8,128)S(1)} %copy-done.78, f32[128,128]{1,0:T(8,128)S(1)} %convolution_negate_fusion.10, f32[128,256]{1,0:T(8,128)S(1)} %copy-done.62, ...), kind=kOutput, calls=%fused_computation.26 | convolution fusion | flops 12894339072 | bytes 9437184 | tf_op jit(solution)/shard_map/dot_general | solution.py:27
  447.2 19.5 %convolution_convert_fusion = bf16[1024,1024]{1,0:T(8,128)(2,1)S(1)} fusion(f32[1024,1024]{1,0:T(8,128)S(1)} %bitcast.196, f32[512,512]{1,0:T(8,128)} %copy-done.28, f32[128,128]{1,0:T(8,128)S(1)} %copy-done.78, f32[128,128]{1,0:T(8,128)S(1)} %convolution_negate_fusion.10, f32[128,256]{1,0:T(8,128)S(1)} %copy-done.62, ...), kind=kOutput, calls=%fused_computation.27 | convolution fusion | flops 12894339072 | bytes 9437184 | tf_op jit(solution)/shard_map/dot_general | solution.py:27
  484.9 11.7 %custom-call.52 = f32[128,128]{1,0:T(8,128)S(1)} custom-call(f32[128,128]{1,0:T(8,128)S(1)} %slice.287), custom_call_target="Cholesky" | custom-call | tf_op jit(solution)/shard_map/cholesky/custom-call.1 | solution.py:39
  516.9 11.9 %custom-call.54 = f32[128,128]{1,0:T(8,128)S(1)} custom-call(f32[128,128]{1,0:T(8,128)S(1)} %slice.290), custom_call_target="Cholesky" | custom-call | tf_op jit(solution)/shard_map/cholesky/custom-call.1 | solution.py:39
  548.3 11.7 %custom-call.56 = f32[128,128]{1,0:T(8,128)S(1)} custom-call(f32[128,128]{1,0:T(8,128)S(1)} %slice.293), custom_call_target="Cholesky" | custom-call | tf_op jit(solution)/shard_map/cholesky/custom-call.1 | solution.py:39
  578.0 11.7 %custom-call.58 = f32[128,128]{1,0:T(8,128)S(1)} custom-call(f32[128,128]{1,0:T(8,128)S(1)} %slice.296), custom_call_target="Cholesky" | custom-call | tf_op jit(solution)/shard_map/cholesky/custom-call.1 | solution.py:39
  608.7 11.9 %custom-call.60 = f32[128,128]{1,0:T(8,128)S(1)} custom-call(f32[128,128]{1,0:T(8,128)S(1)} %slice.299), custom_call_target="Cholesky" | custom-call | tf_op jit(solution)/shard_map/cholesky/custom-call.1 | solution.py:39
  637.2 13.2 %custom-call.62 = f32[128,128]{1,0:T(8,128)} custom-call(f32[128,128]{1,0:T(8,128)} %slice.302), custom_call_target="Cholesky" | custom-call | tf_op jit(solution)/shard_map/cholesky/custom-call.1 | solution.py:39
  654.0 11.5 %custom-call.63 = f32[1,128,128]{1,2,0:T(8,128)} custom-call(f32[1,128,128]{2,1,0:T(8,128)} %get-tuple-element.17), custom_call_target="InvertDiagBlocksLowerTriangular" | custom-call | tf_op jit(solution)/shard_map/jit(_solve_triangular)/triangular_solve | solution.py:40
  673.4 13.2 %custom-call.64 = f32[128,128]{1,0:T(8,128)} custom-call(f32[128,128]{1,0:T(8,128)} %slice.305), custom_call_target="Cholesky" | custom-call | tf_op jit(solution)/shard_map/cholesky/custom-call.1 | solution.py:39
  706.2 13.2 %custom-call.66 = f32[128,128]{1,0:T(8,128)} custom-call(f32[128,128]{1,0:T(8,128)} %convolution_subtract_fusion.7), custom_call_target="Cholesky" | custom-call | tf_op jit(solution)/shard_map/cholesky/custom-call.1 | solution.py:39
  727.8 11.7 %custom-call.67 = f32[1,128,128]{1,2,0:T(8,128)} custom-call(f32[1,128,128]{2,1,0:T(8,128)} %get-tuple-element.13), custom_call_target="InvertDiagBlocksLowerTriangular" | custom-call | tf_op jit(solution)/shard_map/jit(_solve_triangular)/triangular_solve | solution.py:40
  757.8 16.0 %reduce_sum.44 = bf16[3968,1024]{1,0:T(8,128)(2,1)} reduce(bf16[4,3968,1024]{2,1,0:T(8,128)(2,1)} %bitcast.190, bf16[]{:T(256)} %constant.54.clone.1), dimensions={0}, to_apply=%region_4.7 | reduce | flops 12189696 | bytes 40632320 | tf_op jit(solution)/shard_map/reduce_sum | solution.py:13
  773.7 23.1 %bitcast_select_fusion = f32[3968,1024]{1,0:T(8,128)} fusion(f32[1024,3968]{0,1:T(8,128)} %get-tuple-element.63, f32[3968,1024]{1,0:T(8,128)} %bitcast.193, pred[]{:T(512)S(6)} %eq.47, bf16[3968,1024]{1,0:T(8,128)(2,1)} %reduce_sum.44, bf16[1024,1024]{1,0:T(8,128)(2,1)} %fusion.9), kind=kOutput, calls=%fused_computation.2 | convolution fusion | flops 8329625600 | bytes 58982400 | tf_op jit(solution)/shard_map/dot_general | solution.py:107
  796.9 31.3 %convert_select_fusion = (bf16[3840,1024]{1,0:T(8,128)(2,1)}, f32[3840,1024]{1,0:T(8,128)}) fusion(pred[]{:T(512)S(6)} %eq.49, f32[512,512]{1,0:T(8,128)} %select_maximum_fusion.2, f32[128,128]{1,0:T(8,128)} %copy.53, f32[128,128]{1,0:T(8,128)} %copy-done.73, f32[128,256]{1,0:T(8,128)} %concatenate.258, f32[256,256]{1,0:T(8,128)} %copy-done.66, ...), kind=kOutput, calls=%fused_computation.8 | convolution fusion | flops 24175443968 | bytes 42467328 | tf_op jit(solution)/shard_map/dot_general | solution.py:17
  844.0 18.1 %fusion.3 = bf16[1024,1024]{1,0:T(8,128)(2,1)} fusion(f32[1024,1024]{1,0:T(8,128)} %fusion.249, f32[1,1024,1024]{2,1,0:T(8,128)} %all-gather.33.cloned.1.call-done, f32[512,512]{1,0:T(8,128)S(1)} %copy-done.27, f32[128,128]{1,0:T(8,128)S(1)} %copy-done.76, f32[128,128]{1,0:T(8,128)S(1)} %copy-done.74, f32[128,256]{1,0:T(8,128)S(1)} %copy-done.60, ...), kind=kOutput, calls=%fused_computation.13 | convolution fusion | flops 12894339072 | bytes 13631488 | tf_op jit(solution)/shard_map/dot_general | solution.py:27
  863.4 156.1 %all-gather.31.cloned.1.call-done = bf16[15360,1024]{1,0:T(8,128)(2,1)} async-done(((bf16[3840,1024]{1,0:T(8,128)(2,1)}), bf16[15360,1024]{1,0:T(8,128)(2,1)}) %all-gather.31.cloned.1.call-update) | async-done | bytes 31457296 | tf_op jit(solution)/shard_map/all_gather | solution.py:13
  1019.5 15.6 %reduce_sum.45 = bf16[3840,1024]{1,0:T(8,128)(2,1)} reduce(bf16[4,3840,1024]{2,1,0:T(8,128)(2,1)} %bitcast.191, bf16[]{:T(256)} %constant.54.clone.1), dimensions={0}, to_apply=%region_5.8 | reduce | flops 11796480 | bytes 39321600 | tf_op jit(solution)/shard_map/reduce_sum | solution.py:13
  1035.2 20.0 %fusion = f32[3840,1024]{1,0:T(8,128)} fusion(f32[3840,1024]{1,0:T(8,128)} %get-tuple-element.65, f32[3968,1024]{1,0:T(8,128)} %bitcast_select_fusion, bf16[3840,1024]{1,0:T(8,128)(2,1)} %reduce_sum.45, pred[]{:T(512)S(6)} %gt.3, pred[]{:T(512)S(6)} %eq.49, bf16[1024,1024]{1,0:T(8,128)(2,1)S(1)} %copy-done.88), kind=kOutput, calls=%fused_computation.4 | convolution fusion | flops 8064860160 | bytes 57147392 | tf_op jit(solution)/shard_map/dot_general | solution.py:107
  (404 shorter events, 365.7 us)
Async XLA Ops:
  6.5 27.7 %all-gather.17.cloned.1.call-start = ((), (), s32[]{:S(2)}) async-start(), calls=%async_computation | async-start | bytes 2621440 | tf_op jit(solution)/shard_map/all_gather | solution.py:13
  9.1 61.2 %all-gather.21.cloned.1.call-start = ((), (), s32[]{:S(2)}) async-start(), calls=%async_computation.2 | async-start | bytes 5242880 | tf_op jit(solution)/shard_map/all_gather | solution.py:13
  11.5 134.4 %all-gather.19.cloned.1.call-start = ((), (), s32[]{:S(2)}) async-start(), calls=%async_computation.1 | async-start | bytes 4718592 | tf_op jit(solution)/shard_map/all_gather | solution.py:78
  37.1 385.2 %all-gather.23.cloned.1.call-start = ((), (), s32[]{:S(2)}) async-start(), calls=%async_computation.3 | async-start | bytes 4718592 | tf_op jit(solution)/shard_map/all_gather | solution.py:78
  75.0 347.4 %all-gather.25.cloned.1.call-start = ((), (), s32[]{:S(2)}) async-start(), calls=%async_computation.4 | async-start | bytes 4718592 | tf_op jit(solution)/shard_map/all_gather | solution.py:78
  75.6 351.3 %all-gather.29.cloned.1.call-start = ((), (), s32[]{:S(2)}) async-start(), calls=%async_computation.6 | async-start | bytes 4718592 | tf_op jit(solution)/shard_map/all_gather | solution.py:78
  76.2 681.6 %all-gather.27.cloned.1.call-start = ((), (), s32[]{:S(2)}) async-start(), calls=%async_computation.5 | async-start | bytes 40632320 | tf_op jit(solution)/shard_map/all_gather | solution.py:13
  171.1 214.6 %copy-start.40 = (f32[128,128]{1,0:T(8,128)}, f32[128,128]{1,0:T(8,128)S(1)}, u32[]{:S(2)}) copy-start(f32[128,128]{1,0:T(8,128)S(1)} %get-tuple-element.44) | copy-start | bytes 196612
  202.7 180.1 %copy-start.41 = (f32[128,128]{1,0:T(8,128)}, f32[128,128]{1,0:T(8,128)S(1)}, u32[]{:S(2)}) copy-start(f32[128,128]{1,0:T(8,128)S(1)} %get-tuple-element.42) | copy-start | bytes 196612
  276.4 23.6 %copy-start.12 = (f32[512,512]{1,0:T(8,128)}, f32[512,512]{1,0:T(8,128)S(1)}, u32[]{:S(2)}) copy-start(f32[512,512]{1,0:T(8,128)S(1)} %convolution_subtract_fusion.2) | copy-start | bytes 3145732
  317.3 67.3 %copy-start.37 = (f32[128,128]{1,0:T(8,128)}, f32[128,128]{1,0:T(8,128)S(1)}, u32[]{:S(2)}) copy-start(f32[128,128]{1,0:T(8,128)S(1)} %get-tuple-element.34) | copy-start | bytes 196612
  327.5 27.1 %copy-start.50 = (f32[128,128]{1,0:T(8,128)}, f32[128,128]{1,0:T(8,128)S(1)}, u32[]{:S(2)}) copy-start(f32[128,128]{1,0:T(8,128)S(1)} %copy.36) | copy-start | bytes 196612
  329.2 27.0 %copy-start.47 = (f32[128,128]{1,0:T(8,128)}, f32[128,128]{1,0:T(8,128)S(1)}, u32[]{:S(2)}) copy-start(f32[128,128]{1,0:T(8,128)S(1)} %convolution_negate_fusion.11) | copy-start | bytes 196612
  355.3 28.0 %copy-start.51 = (f32[128,128]{1,0:T(8,128)S(1)}, f32[128,128]{1,0:T(8,128)}, u32[]{:S(2)}) copy-start(f32[128,128]{1,0:T(8,128)} %copy-done.50) | copy-start | bytes 196612
  357.1 30.5 %copy-start.17 = (f32[128,128]{1,0:T(8,128)}, f32[128,128]{1,0:T(8,128)S(1)}, u32[]{:S(2)}) copy-start(f32[128,128]{1,0:T(8,128)S(1)} %fusion.208) | copy-start | bytes 196612
  426.1 417.9 %all-gather.33.cloned.1.call-start = ((), (), s32[]{:S(2)}) async-start(), calls=%async_computation.8 | async-start | bytes 4718592 | tf_op jit(solution)/shard_map/all_gather | solution.py:78
  426.9 592.7 %all-gather.31.cloned.1.call-start = ((), (), s32[]{:S(2)}) async-start(), calls=%async_computation.7 | async-start | bytes 39321600 | tf_op jit(solution)/shard_map/all_gather | solution.py:13
  427.0 20.2 %copy-start.83 = (f32[1,1024,1024]{2,1,0:T(8,128)S(1)}, f32[1,1024,1024]{2,1,0:T(8,128)}, u32[]{:S(2)}) copy-start(f32[1,1024,1024]{2,1,0:T(8,128)} %all-gather.25.cloned.1.call-done) | copy-start | bytes 12582916
  427.0 20.2 %copy-start.85 = (f32[512,512]{1,0:T(8,128)S(1)}, f32[512,512]{1,0:T(8,128)}, u32[]{:S(2)}) copy-start(f32[512,512]{1,0:T(8,128)} %copy-done.84) | copy-start | bytes 3145732
  447.2 20.9 %copy-start.82 = (f32[1,1024,1024]{1,2,0:T(8,128)S(1)}, f32[1,1024,1024]{1,2,0:T(8,128)}, u32[]{:S(2)}) copy-start(f32[1,1024,1024]{1,2,0:T(8,128)} %all-gather.23.cloned.1.call-done) | copy-start | bytes 12582916
  540.9 35.9 %copy-start.32 = (f32[128,128]{0,1:T(8,128)}, f32[128,128]{0,1:T(8,128)S(1)}, u32[]{:S(2)}) copy-start(f32[128,128]{0,1:T(8,128)S(1)} %fusion.100) | copy-start | bytes 196612
  572.4 35.2 %copy-start.31 = (f32[128,128]{1,0:T(8,128)}, f32[128,128]{1,0:T(8,128)S(1)}, u32[]{:S(2)}) copy-start(f32[128,128]{1,0:T(8,128)S(1)} %fusion.98) | copy-start | bytes 196612
  601.8 30.6 %copy-start.29 = (f32[128,128]{0,1:T(8,128)}, f32[128,128]{0,1:T(8,128)S(1)}, u32[]{:S(2)}) copy-start(f32[128,128]{0,1:T(8,128)S(1)} %fusion.96) | copy-start | bytes 196612
  742.8 8.3 copy-start.10
  742.8 8.3 copy-start.24
  742.8 8.3 copy-start.35
  742.8 8.3 copy-start.44
  742.8 8.3 copy-start.45
  742.8 8.3 copy-start.64
  742.8 8.3 copy-start.70
  742.8 8.3 copy-start.80
  1019.5 15.6 %copy-start.88 = (bf16[1024,1024]{1,0:T(8,128)(2,1)S(1)}, bf16[1024,1024]{1,0:T(8,128)(2,1)}, u32[]{:S(2)}) copy-start(bf16[1024,1024]{1,0:T(8,128)(2,1)} %fusion.3) | copy-start | bytes 6291460
  (67 other events, 224.6 us)
Sparse Core Ops, SparseCore 0:
  9.2 25.0 all-gather.16
  35.8 34.4 all-gather.20
  72.4 73.4 all-gather.18
  147.8 73.1 all-gather.22
  223.0 70.5 all-gather.24
  295.6 71.9 all-gather.28
  426.2 197.5 all-gather.26
  626.0 71.9 all-gather.32
  828.3 191.1 all-gather.30
